TPU v7x, 32 devices: a whole 2x2x4 slice. The times are simulated.
32 devices in a mesh: lvl: 8 (over z, y), lon: 4 (over x, core).
Axes of the slice: x: 2, y: 2, z: 4, core: 2. Of those that a mesh axis runs over, the one named last changes fastest.
Arguments:
- window: float32 [8, 16, 69, 512], P('lvl', None, None, 'lon'), may hold values from -6 to 6
- anchor: float32 [16, 69, 512], P(None, None, 'lon'), may hold values from -6 to 6
- noise: float32 [8, 16, 69, 512], P('lvl', None, None, 'lon'), may hold values from -6 to 6
- conv_in: bfloat16 [3, 3, 192, 69], replicated, may hold values from -0.25 to 0.25
- conv_out: bfloat16 [3, 3, 69, 192], replicated, may hold values from -0.15625 to 0.15625
- time_shift: float32 [192], replicated, may hold values from -4 to 4
- plan: int32 [256], replicated, may hold values from 0 to 999, as said below
- start: int32 [1], replicated, may hold values from 0 to 247
Outputs:
- advanced: float32 [8, 16, 69, 512], P('lvl', None, None, 'lon')
Inputs may be any that keep to these rules, and one draw needn't show every extreme that they name: `plan`: strictly decreasing, first entry 999.
All inputs are finite; a program needn't handle non-finite values.
Results may differ from a plain program's by a relative error of at most 0.0003.
Values may be sent and summed in bfloat16 or wider, within the bound.
No kernel may reach another device: no remote copies, remote signals or barrier semaphores. Data moves between devices by JAX's collectives and lax.ppermute only.
A program may use at most 64 MiB of HBM per device.

v0:
```python
import jax
import jax.numpy as jnp
from jax import lax
from jax.sharding import PartitionSpec as P

SWEEPS = 2


def extended(block, sides, width):
    for axis, dim in sides:
        count = lax.axis_size(axis)
        forward = [(i, i + 1) for i in range(count - 1)]
        forward.append((count - 1, 0))
        backward = [(target, source) for source, target in forward]
        low = lax.ppermute(
            lax.slice_in_dim(block, block.shape[dim] - width, None, axis=dim), axis, forward
        )
        high = lax.ppermute(lax.slice_in_dim(block, 0, width, axis=dim), axis, backward)
        block = jnp.concatenate([low, block, high], axis=dim)
    return block


def convolve(padded, weight, width_out):
    rows = padded.shape[1] - 2
    total = jnp.zeros((padded.shape[0], rows, weight.shape[2], width_out), jnp.float32)
    for a in range(3):
        for b in range(3):
            piece = padded[:, a : a + rows, :, b : b + width_out]
            total = total + jnp.einsum(
                "oc,vlcn->vlon", weight[a, b], piece, preferred_element_type=jnp.float32
            )
    return total


def pad_rows(field):
    return jnp.pad(field, ((0, 0), (1, 1), (0, 0), (0, 0)))


def exclusive_sum(values):
    running = jnp.cumsum(values, axis=0)
    return jnp.concatenate([jnp.zeros_like(values[:1]), running[:-1]], axis=0)


def body(window, anchor, noise, conv_in, conv_out, time_shift, plan, start):
    levels_here = window.shape[0]
    width = window.shape[3]
    offset = start[0] + lax.axis_index("lvl") * levels_here
    times = lax.dynamic_slice(plan, (offset,), (levels_here + 1,)).astype(jnp.float32)
    t_now = times[:-1]
    beta = 0.1 + 19.9 * t_now / 1000.0
    step = (t_now - times[1:]) / 1000.0
    beta_col = beta[:, None, None, None]
    step_col = step[:, None, None, None]
    spread = jnp.sqrt(beta * step)[:, None, None, None] * noise
    shift = (t_now / 1000.0)[:, None, None, None] * time_shift[None, None, :, None]
    states = window
    inclusive = None
    for sweep in range(SWEEPS):
        rounded = states.astype(jnp.bfloat16)
        rimmed = extended(rounded, (("lon", 3),), 1)
        pre = convolve(pad_rows(rimmed), conv_in, width)
        hidden = jax.nn.silu(pre + shift).astype(jnp.bfloat16)
        hidden_wide = extended(hidden, (("lon", 3),), 1)
        score = convolve(pad_rows(hidden_wide), conv_out, width)
        increment = (0.5 * beta_col * states + beta_col * score) * step_col + spread
        earlier = exclusive_sum(
            lax.all_to_all(increment, "lvl", split_axis=1, concat_axis=0, tiled=True)
        )
        before = lax.all_to_all(earlier, "lvl", split_axis=0, concat_axis=1, tiled=True)
        inclusive = before + increment
        states = anchor[None] + before
    return anchor[None] + inclusive


def solution(mesh):
    return jax.shard_map(
        body,
        mesh=mesh,
        in_specs=(
            P("lvl", None, None, "lon"),
            P(None, None, "lon"),
            P("lvl", None, None, "lon"),
            P(),
            P(),
            P(),
            P(),
            P(),
        ),
        out_specs=P("lvl", None, None, "lon"),
        check_vma=False,
    )
```

profile of v0, /device:TPU:0, one launch (start us, length us, event | category | flops | bytes accessed | tf_op | source)
XLA Modules:
  0.0 134.5 jit_solution(6368105280167487864)
XLA Ops:
  0.0 1.3 copy.76
  1.5 0.5 collective-permute-start
  2.0 2.0 %collective-permute-start.1 = (bf16[1,16,69,1]{3,2,1,0:T(8,128)(2,1)S(1)}, bf16[1,16,69,1]{3,2,1,0:T(8,128)(2,1)S(1)}, u32[]{:S(2)}, u32[]{:S(2)}) collective-permute-start(bf16[1,16,69,1]{3,2,1,0:T(8,128)(2,1)S(1)} %get-tuple-element.14), channel_id=1, source_target_pairs={{1,0},{2,1},{3,2},{0,3},{5,4},{6,5},{7,6},{4,7},{9,8},{10,9},{11,1... | collective-permute-start | bytes 6632 | tf_op jit(solution)/shard_map/ppermute | solution.py:18
  4.7 0.6 fusion.153
  6.4 2.4 %collective-permute-done = bf16[1,16,69,1]{3,2,1,0:T(8,128)(2,1)S(1)} collective-permute-done((bf16[1,16,69,1]{3,2,1,0:T(8,128)(2,1)S(1)}, bf16[1,16,69,1]{3,2,1,0:T(8,128)(2,1)S(1)}, u32[]{:S(2)}, u32[]{:S(2)}) %collective-permute-start) | collective-permute-done | bytes 2240 | tf_op jit(solution)/shard_map/ppermute | solution.py:15
  8.9 2.4 %collective-permute-done.1 = bf16[1,16,69,1]{3,2,1,0:T(8,128)(2,1)S(1)} collective-permute-done((bf16[1,16,69,1]{3,2,1,0:T(8,128)(2,1)S(1)}, bf16[1,16,69,1]{3,2,1,0:T(8,128)(2,1)S(1)}, u32[]{:S(2)}, u32[]{:S(2)}) %collective-permute-start.1) | collective-permute-done | bytes 2240 | tf_op jit(solution)/shard_map/ppermute | solution.py:18
  11.7 0.5 fusion.53
  12.6 0.5 fusion.62
  13.0 0.5 fusion.63
  13.9 0.5 fusion.52
  14.4 0.5 fusion.59
  14.9 1.2 fusion.8
  17.2 2.3 %collective-permute-start.3 = (bf16[1,16,192,1]{2,1,3,0:T(8,128)(2,1)S(1)}, bf16[1,16,192,1]{2,1,3,0:T(8,128)(2,1)S(1)}, u32[]{:S(2)}, u32[]{:S(2)}) collective-permute-start(bf16[1,16,192,1]{2,1,3,0:T(8,128)(2,1)S(1)} %copy.43), channel_id=1, source_target_pairs={{1,0},{2,1},{3,2},{0,3},{5,4},{6,5},{7,6},{4,7},{9,8},{10,9},{11,1... | collective-permute-start | bytes 18440 | tf_op jit(solution)/shard_map/ppermute | solution.py:18
  21.6 0.4 copy.44
  22.0 0.4 copy.45
  22.5 0.9 select_maximum_fusion.2
  23.5 0.5 fusion.34
  24.2 0.5 convolution_add_fusion.14
  24.7 0.5 convolution_add_fusion.13
  25.5 0.7 convolution_add_fusion.11
  26.5 0.5 convolution_add_fusion.9
  27.4 0.6 fusion.17
  28.1 0.6 copy.49
  28.6 22.1 %all_to_all.48 = f32[1,16,69,128]{3,0,2,1:T(1,128)S(1)} all-to-all(f32[1,16,69,128]{3,0,2,1:T(1,128)S(1)} %copy.49), channel_id=1, replica_groups=mesh['lvl'=8,'lon'=4] {'lvl'}, dimensions={1} | all-to-all | bytes 1130496 | tf_op jit(solution)/shard_map/all_to_all | solution.py:67
  51.4 18.8 %all_to_all.49 = f32[8,2,69,128]{3,1,2,0:T(2,128)S(1)} all-to-all(f32[8,2,69,128]{3,1,2,0:T(2,128)S(1)} %concatenate.48.clone), channel_id=1, replica_groups=mesh['lvl'=8,'lon'=4] {'lvl'}, dimensions={0} | all-to-all | bytes 1130496 | tf_op jit(solution)/shard_map/all_to_all | solution.py:69
  70.7 1.7 %collective-permute-start.5 = (bf16[1,16,69,1]{3,2,1,0:T(8,128)(2,1)S(1)}, bf16[1,16,69,1]{3,2,1,0:T(8,128)(2,1)S(1)}, u32[]{:S(2)}, u32[]{:S(2)}) collective-permute-start(bf16[1,16,69,1]{3,2,1,0:T(8,128)(2,1)S(1)} %get-tuple-element.12), channel_id=1, source_target_pairs={{1,0},{2,1},{3,2},{0,3},{5,4},{6,5},{7,6},{4,7},{9,8},{10,9},{11,1... | collective-permute-start | bytes 6632 | tf_op jit(solution)/shard_map/ppermute | solution.py:18
  72.9 6.7 %collective-permute-done.4 = bf16[1,16,69,1]{3,2,1,0:T(8,128)(2,1)S(1)} collective-permute-done((bf16[1,16,69,1]{3,2,1,0:T(8,128)(2,1)S(1)}, bf16[1,16,69,1]{3,2,1,0:T(8,128)(2,1)S(1)}, u32[]{:S(2)}, u32[]{:S(2)}) %collective-permute-start.4) | collective-permute-done | bytes 2240 | tf_op jit(solution)/shard_map/ppermute | solution.py:15
  79.9 0.5 fusion.40
  80.8 0.5 fusion.49
  81.3 0.5 fusion.50
  82.2 0.5 fusion.39
  82.6 0.5 fusion.46
  83.1 1.2 fusion.9
  85.7 1.5 %collective-permute-start.7 = (bf16[1,16,192,1]{2,1,3,0:T(8,128)(2,1)S(1)}, bf16[1,16,192,1]{2,1,3,0:T(8,128)(2,1)S(1)}, u32[]{:S(2)}, u32[]{:S(2)}) collective-permute-start(bf16[1,16,192,1]{2,1,3,0:T(8,128)(2,1)S(1)} %copy.55), channel_id=1, source_target_pairs={{1,0},{2,1},{3,2},{0,3},{5,4},{6,5},{7,6},{4,7},{9,8},{10,9},{11,1... | collective-permute-start | bytes 18440 | tf_op jit(solution)/shard_map/ppermute | solution.py:18
  87.2 0.9 collective-permute-done.6
  88.1 0.4 copy.56
  88.6 0.4 copy.57
  89.0 0.9 select_maximum_fusion
  90.0 0.5 fusion.27
  90.7 0.5 convolution_add_fusion.6
  91.2 0.5 convolution_add_fusion.5
  92.0 0.7 convolution_add_fusion.3
  93.0 0.5 convolution_add_fusion.1
  93.4 0.5 fusion.20
  94.0 0.6 copy.60
  94.6 19.2 %all_to_all.50 = f32[1,16,69,128]{3,0,2,1:T(1,128)S(1)} all-to-all(f32[1,16,69,128]{3,0,2,1:T(1,128)S(1)} %copy.60), channel_id=1, replica_groups=mesh['lvl'=8,'lon'=4] {'lvl'}, dimensions={1} | all-to-all | bytes 1130496 | tf_op jit(solution)/shard_map/all_to_all | solution.py:67
  114.5 18.8 %all_to_all.51 = f32[8,2,69,128]{3,1,2,0:T(2,128)S(1)} all-to-all(f32[8,2,69,128]{3,1,2,0:T(2,128)S(1)} %concatenate.55.clone), channel_id=1, replica_groups=mesh['lvl'=8,'lon'=4] {'lvl'}, dimensions={0} | all-to-all | bytes 1130496 | tf_op jit(solution)/shard_map/all_to_all | solution.py:69
  133.6 0.9 copy.64
  (65 shorter events, 10.2 us)
Async XLA Ops:
  0.0 4.6 %copy-start.9 = (s32[256]{0:T(256)S(1)}, s32[256]{0:T(256)}, u32[]{:S(2)}) copy-start(s32[256]{0:T(256)} %param.14) | copy-start | bytes 3076
  0.0 5.3 %copy-start.6 = (bf16[3,3,192,69]{2,3,1,0:T(8,128)(2,1)S(1)}, bf16[3,3,192,69]{2,3,1,0:T(8,128)(2,1)}, u32[]{:S(2)}) copy-start(bf16[3,3,192,69]{2,3,1,0:T(8,128)(2,1)} %param.11) | copy-start | bytes 715396
  1.3 5.1 %copy-start.8 = (f32[192]{0:T(256)S(1)}, f32[192]{0:T(256)}, u32[]{:S(2)}) copy-start(f32[192]{0:T(256)} %param.13) | copy-start | bytes 2308
  1.5 7.4 %collective-permute-start = (bf16[1,16,69,1]{3,2,1,0:T(8,128)(2,1)S(1)}, bf16[1,16,69,1]{3,2,1,0:T(8,128)(2,1)S(1)}, u32[]{:S(2)}, u32[]{:S(2)}) collective-permute-start(bf16[1,16,69,1]{3,2,1,0:T(8,128)(2,1)S(1)} %get-tuple-element.13), channel_id=1, source_target_pairs={{0,1},{1,2},{2,3},{3,0},{4,5},{5,6},{6,7},{7,4},{8,9},{9,10},{10,1... | collective-permute-start | bytes 6632 | tf_op jit(solution)/shard_map/ppermute | solution.py:15
  2.0 9.3 %collective-permute-start.1 = (bf16[1,16,69,1]{3,2,1,0:T(8,128)(2,1)S(1)}, bf16[1,16,69,1]{3,2,1,0:T(8,128)(2,1)S(1)}, u32[]{:S(2)}, u32[]{:S(2)}) collective-permute-start(bf16[1,16,69,1]{3,2,1,0:T(8,128)(2,1)S(1)} %get-tuple-element.14), channel_id=1, source_target_pairs={{1,0},{2,1},{3,2},{0,3},{5,4},{6,5},{7,6},{4,7},{9,8},{10,9},{11,1... | collective-permute-start | bytes 6632 | tf_op jit(solution)/shard_map/ppermute | solution.py:18
  16.8 4.8 %collective-permute-start.2 = (bf16[1,16,192,1]{2,1,3,0:T(8,128)(2,1)S(1)}, bf16[1,16,192,1]{2,1,3,0:T(8,128)(2,1)S(1)}, u32[]{:S(2)}, u32[]{:S(2)}) collective-permute-start(bf16[1,16,192,1]{2,1,3,0:T(8,128)(2,1)S(1)} %copy.42), channel_id=1, source_target_pairs={{0,1},{1,2},{2,3},{3,0},{4,5},{5,6},{6,7},{7,4},{8,9},{9,10},{10,1... | collective-permute-start | bytes 18440 | tf_op jit(solution)/shard_map/ppermute | solution.py:15
  17.2 4.8 %collective-permute-start.3 = (bf16[1,16,192,1]{2,1,3,0:T(8,128)(2,1)S(1)}, bf16[1,16,192,1]{2,1,3,0:T(8,128)(2,1)S(1)}, u32[]{:S(2)}, u32[]{:S(2)}) collective-permute-start(bf16[1,16,192,1]{2,1,3,0:T(8,128)(2,1)S(1)} %copy.43), channel_id=1, source_target_pairs={{1,0},{2,1},{3,2},{0,3},{5,4},{6,5},{7,6},{4,7},{9,8},{10,9},{11,1... | collective-permute-start | bytes 18440 | tf_op jit(solution)/shard_map/ppermute | solution.py:18
  22.5 1.0 copy-start.4
  26.2 1.1 copy-start
  26.2 1.2 copy-start.1
  51.2 19.0 %copy-start.2 = (f32[16,69,128]{2,0,1:T(8,128)S(1)}, f32[16,69,128]{2,0,1:T(8,128)}, u32[]{:S(2)}) copy-start(f32[16,69,128]{2,0,1:T(8,128)} %param.9) | copy-start | bytes 1695748
  70.3 2.2 %copy-start.7 = (bf16[3,3,192,69]{2,3,1,0:T(8,128)(2,1)S(1)}, bf16[3,3,192,69]{2,3,1,0:T(8,128)(2,1)}, u32[]{:S(2)}) copy-start(bf16[3,3,192,69]{2,3,1,0:T(8,128)(2,1)} %param.11) | copy-start | bytes 715396
  70.7 8.9 %collective-permute-start.4 = (bf16[1,16,69,1]{3,2,1,0:T(8,128)(2,1)S(1)}, bf16[1,16,69,1]{3,2,1,0:T(8,128)(2,1)S(1)}, u32[]{:S(2)}, u32[]{:S(2)}) collective-permute-start(bf16[1,16,69,1]{3,2,1,0:T(8,128)(2,1)S(1)} %get-tuple-element.11), channel_id=1, source_target_pairs={{0,1},{1,2},{2,3},{3,0},{4,5},{5,6},{6,7},{7,4},{8,9},{9,10},{10,1... | collective-permute-start | bytes 6632 | tf_op jit(solution)/shard_map/ppermute | solution.py:15
  70.7 8.8 %collective-permute-start.5 = (bf16[1,16,69,1]{3,2,1,0:T(8,128)(2,1)S(1)}, bf16[1,16,69,1]{3,2,1,0:T(8,128)(2,1)S(1)}, u32[]{:S(2)}, u32[]{:S(2)}) collective-permute-start(bf16[1,16,69,1]{3,2,1,0:T(8,128)(2,1)S(1)} %get-tuple-element.12), channel_id=1, source_target_pairs={{1,0},{2,1},{3,2},{0,3},{5,4},{6,5},{7,6},{4,7},{9,8},{10,9},{11,1... | collective-permute-start | bytes 6632 | tf_op jit(solution)/shard_map/ppermute | solution.py:18
  85.0 3.1 %collective-permute-start.6 = (bf16[1,16,192,1]{2,1,3,0:T(8,128)(2,1)S(1)}, bf16[1,16,192,1]{2,1,3,0:T(8,128)(2,1)S(1)}, u32[]{:S(2)}, u32[]{:S(2)}) collective-permute-start(bf16[1,16,192,1]{2,1,3,0:T(8,128)(2,1)S(1)} %copy.54), channel_id=1, source_target_pairs={{0,1},{1,2},{2,3},{3,0},{4,5},{5,6},{6,7},{7,4},{8,9},{9,10},{10,1... | collective-permute-start | bytes 18440 | tf_op jit(solution)/shard_map/ppermute | solution.py:15
  85.7 2.8 %collective-permute-start.7 = (bf16[1,16,192,1]{2,1,3,0:T(8,128)(2,1)S(1)}, bf16[1,16,192,1]{2,1,3,0:T(8,128)(2,1)S(1)}, u32[]{:S(2)}, u32[]{:S(2)}) collective-permute-start(bf16[1,16,192,1]{2,1,3,0:T(8,128)(2,1)S(1)} %copy.55), channel_id=1, source_target_pairs={{1,0},{2,1},{3,2},{0,3},{5,4},{6,5},{7,6},{4,7},{9,8},{10,9},{11,1... | collective-permute-start | bytes 18440 | tf_op jit(solution)/shard_map/ppermute | solution.py:18
  89.0 1.0 copy-start.5
  114.3 19.0 %copy-start.3 = (f32[16,69,128]{2,0,1:T(8,128)S(1)}, f32[16,69,128]{2,0,1:T(8,128)}, u32[]{:S(2)}) copy-start(f32[16,69,128]{2,0,1:T(8,128)} %param.9) | copy-start | bytes 1695748
where the time goes:
time: 135 us
  blocking collectives  78.9 us (58%)
  matrix products  17.5 us (13%)
  waiting for transfers between devices  12.5 us (9%)
  local copies, waits for them, and re-layouts  9.75 us (7%)
  starting transfers between devices  8.49 us (6%)
  between operations  3.93 us (3%)
  other arithmetic  3.51 us (3%)
    all_to_all x2, blocking collectives, body(): lax.all_to_all(increment, 'lvl', split_axis=1, concat_axis=0, tiled=True)  41.3 us
    all_to_all x2, blocking collectives, body(): lax.all_to_all(earlier, 'lvl', split_axis=0, concat_axis=1, tiled=True)  37.6 us
    dot_general x36, matrix products, convolve(): jnp.einsum('oc,vlcn->vlon', weight[a, b], piece, preferred_element_type=j...  17.5 us
    ppermute x4, waiting for transfers between devices, extended(): lax.ppermute(lax.slice_in_dim(block, block.shape[dim] - width, None, axis...  10 us
    ppermute x4, starting transfers between devices, extended(): lax.ppermute(lax.slice_in_dim(block, 0, width, axis=dim), axis, backward)  7.5 us
  transfers between devices with their start and end apart: 8, of which 4 were waited for; matrix products, arithmetic and copies ran while one was open for 2% of the time, Pallas kernels for 0%

commit v1 on v0

--- a/solution.py
+++ b/solution.py
@@ -4,6 +4,12 @@
 from jax.sharding import PartitionSpec as P
 
 SWEEPS = 2
+
+
+def stacked_exchange(x, mesh_axis, split, join):
+    parts = jnp.split(x, lax.axis_size(mesh_axis), axis=split)
+    received = lax.all_to_all(jnp.stack(parts), mesh_axis, 0, 0)
+    return jnp.concatenate(received, axis=join)
 
 
 def extended(block, sides, width):
@@ -63,9 +69,7 @@
         hidden_wide = extended(hidden, (("lon", 3),), 1)
         score = convolve(pad_rows(hidden_wide), conv_out, width)
         increment = (0.5 * beta_col * states + beta_col * score) * step_col + spread
-        earlier = exclusive_sum(
-            lax.all_to_all(increment, "lvl", split_axis=1, concat_axis=0, tiled=True)
-        )
+        earlier = exclusive_sum(stacked_exchange(increment, "lvl", 1, 0))
         before = lax.all_to_all(earlier, "lvl", split_axis=0, concat_axis=1, tiled=True)
         inclusive = before + increment
         states = anchor[None] + before

time: 135 us -> 134 us (level)
  transfers between devices with their start and end apart: 8 -> 8, of which waited for: 4 -> 5; matrix products, arithmetic and copies ran while one was open for 2% -> 2% of each run, Pallas kernels for 0% -> 0%
where the time goes in v1:
time: 134 us
  blocking collectives  78.9 us (59%)
  matrix products  17.5 us (13%)
  waiting for transfers between devices  12.5 us (9%)
  local copies, waits for them, and re-layouts  8.81 us (7%)
  starting transfers between devices  8.53 us (6%)
  between operations  4.02 us (3%)
  other arithmetic  3.56 us (3%)
    all_to_all x2, blocking collectives, stacked_exchange(): received = lax.all_to_all(jnp.stack(parts), mesh_axis, 0, 0)  41.3 us
    all_to_all x2, blocking collectives, body(): lax.all_to_all(earlier, 'lvl', split_axis=0, concat_axis=1, tiled=True)  37.6 us
    dot_general x36, matrix products, convolve(): jnp.einsum('oc,vlcn->vlon', weight[a, b], piece, preferred_element_type=j...  17.5 us
    ppermute x4, waiting for transfers between devices, extended(): lax.ppermute(lax.slice_in_dim(block, block.shape[dim] - width, None, axis...  9.83 us
    ppermute x4, starting transfers between devices, extended(): lax.ppermute(lax.slice_in_dim(block, 0, width, axis=dim), axis, backward)  7.54 us
  transfers between devices with their start and end apart: 8, of which 5 were waited for; matrix products, arithmetic and copies ran while one was open for 2% of the time, Pallas kernels for 0%

profile of v1, /device:TPU:0, one launch (start us, length us, event | category | flops | bytes accessed | tf_op | source)
XLA Modules:
  0.0 133.8 jit_solution(5981259884612654695)
XLA Ops:
  0.0 1.3 copy.46
  1.5 0.5 collective-permute-start
  2.0 2.0 %collective-permute-start.1 = (bf16[1,16,69,1]{3,2,1,0:T(8,128)(2,1)S(1)}, bf16[1,16,69,1]{3,2,1,0:T(8,128)(2,1)S(1)}, u32[]{:S(2)}, u32[]{:S(2)}) collective-permute-start(bf16[1,16,69,1]{3,2,1,0:T(8,128)(2,1)S(1)} %get-tuple-element.14), channel_id=1, source_target_pairs={{1,0},{2,1},{3,2},{0,3},{5,4},{6,5},{7,6},{4,7},{9,8},{10,9},{11,1... | collective-permute-start | bytes 6632 | tf_op jit(solution)/shard_map/ppermute | solution.py:24
  4.7 0.6 fusion.173
  6.4 2.4 %collective-permute-done = bf16[1,16,69,1]{3,2,1,0:T(8,128)(2,1)S(1)} collective-permute-done((bf16[1,16,69,1]{3,2,1,0:T(8,128)(2,1)S(1)}, bf16[1,16,69,1]{3,2,1,0:T(8,128)(2,1)S(1)}, u32[]{:S(2)}, u32[]{:S(2)}) %collective-permute-start) | collective-permute-done | bytes 2240 | tf_op jit(solution)/shard_map/ppermute | solution.py:21
  8.9 2.4 %collective-permute-done.1 = bf16[1,16,69,1]{3,2,1,0:T(8,128)(2,1)S(1)} collective-permute-done((bf16[1,16,69,1]{3,2,1,0:T(8,128)(2,1)S(1)}, bf16[1,16,69,1]{3,2,1,0:T(8,128)(2,1)S(1)}, u32[]{:S(2)}, u32[]{:S(2)}) %collective-permute-start.1) | collective-permute-done | bytes 2240 | tf_op jit(solution)/shard_map/ppermute | solution.py:24
  11.7 0.5 fusion.57
  12.6 0.5 fusion.66
  13.0 0.5 fusion.67
  13.5 0.4 fusion.68
  13.9 0.5 fusion.56
  14.4 0.5 fusion.63
  14.9 1.2 fusion.8
  17.2 2.1 %collective-permute-start.3 = (bf16[1,16,192,1]{2,1,3,0:T(8,128)(2,1)S(1)}, bf16[1,16,192,1]{2,1,3,0:T(8,128)(2,1)S(1)}, u32[]{:S(2)}, u32[]{:S(2)}) collective-permute-start(bf16[1,16,192,1]{2,1,3,0:T(8,128)(2,1)S(1)} %copy.19), channel_id=1, source_target_pairs={{1,0},{2,1},{3,2},{0,3},{5,4},{6,5},{7,6},{4,7},{9,8},{10,9},{11,1... | collective-permute-start | bytes 18440 | tf_op jit(solution)/shard_map/ppermute | solution.py:24
  21.4 0.4 copy.20
  21.9 0.4 copy.21
  22.3 0.9 select_maximum_fusion.2
  23.3 0.5 fusion.34
  24.0 0.5 convolution_add_fusion.14
  24.5 0.5 convolution_add_fusion.13
  25.3 0.7 convolution_add_fusion.11
  26.3 0.5 convolution_add_fusion.9
  27.2 0.6 fusion.17
  28.3 22.1 %all_to_all.34 = f32[8,1,2,69,128]{4,2,3,1,0:T(2,128)S(1)} all-to-all(f32[8,1,2,69,128]{4,2,3,1,0:T(2,128)S(1)} %copy.25), channel_id=1, replica_groups=mesh['lvl'=8,'lon'=4] {'lvl'}, dimensions={0} | all-to-all | bytes 1130496 | tf_op jit(solution)/shard_map/all_to_all | solution.py:11
  50.9 18.8 %all_to_all.35 = f32[8,2,69,128]{3,1,2,0:T(2,128)S(1)} all-to-all(f32[8,2,69,128]{3,1,2,0:T(2,128)S(1)} %concatenate.48), channel_id=1, replica_groups=mesh['lvl'=8,'lon'=4] {'lvl'}, dimensions={0} | all-to-all | bytes 1130496 | tf_op jit(solution)/shard_map/all_to_all | solution.py:73
  70.1 1.7 %collective-permute-start.5 = (bf16[1,16,69,1]{3,2,1,0:T(8,128)(2,1)S(1)}, bf16[1,16,69,1]{3,2,1,0:T(8,128)(2,1)S(1)}, u32[]{:S(2)}, u32[]{:S(2)}) collective-permute-start(bf16[1,16,69,1]{3,2,1,0:T(8,128)(2,1)S(1)} %get-tuple-element.12), channel_id=1, source_target_pairs={{1,0},{2,1},{3,2},{0,3},{5,4},{6,5},{7,6},{4,7},{9,8},{10,9},{11,1... | collective-permute-start | bytes 6632 | tf_op jit(solution)/shard_map/ppermute | solution.py:24
  72.3 6.7 %collective-permute-done.4 = bf16[1,16,69,1]{3,2,1,0:T(8,128)(2,1)S(1)} collective-permute-done((bf16[1,16,69,1]{3,2,1,0:T(8,128)(2,1)S(1)}, bf16[1,16,69,1]{3,2,1,0:T(8,128)(2,1)S(1)}, u32[]{:S(2)}, u32[]{:S(2)}) %collective-permute-start.4) | collective-permute-done | bytes 2240 | tf_op jit(solution)/shard_map/ppermute | solution.py:21
  79.3 0.5 fusion.44
  79.8 0.4 fusion.45
  80.2 0.5 fusion.53
  80.7 0.5 fusion.54
  81.6 0.5 fusion.43
  82.1 0.5 fusion.50
  82.5 1.2 fusion.9
  85.1 1.7 %collective-permute-start.7 = (bf16[1,16,192,1]{2,1,3,0:T(8,128)(2,1)S(1)}, bf16[1,16,192,1]{2,1,3,0:T(8,128)(2,1)S(1)}, u32[]{:S(2)}, u32[]{:S(2)}) collective-permute-start(bf16[1,16,192,1]{2,1,3,0:T(8,128)(2,1)S(1)} %copy.29), channel_id=1, source_target_pairs={{1,0},{2,1},{3,2},{0,3},{5,4},{6,5},{7,6},{4,7},{9,8},{10,9},{11,1... | collective-permute-start | bytes 18440 | tf_op jit(solution)/shard_map/ppermute | solution.py:24
  86.8 0.7 collective-permute-done.6
  87.5 0.4 copy.30
  88.2 0.4 copy.31
  88.7 0.9 select_maximum_fusion
  89.6 0.5 fusion.27
  90.4 0.5 convolution_add_fusion.6
  90.8 0.5 convolution_add_fusion.5
  91.6 0.7 convolution_add_fusion.3
  92.6 0.5 convolution_add_fusion.1
  93.1 0.5 fusion.20
  94.1 19.2 %all_to_all.36 = f32[8,1,2,69,128]{4,2,3,1,0:T(2,128)S(1)} all-to-all(f32[8,1,2,69,128]{4,2,3,1,0:T(2,128)S(1)} %copy.34), channel_id=1, replica_groups=mesh['lvl'=8,'lon'=4] {'lvl'}, dimensions={0} | all-to-all | bytes 1130496 | tf_op jit(solution)/shard_map/all_to_all | solution.py:11
  113.8 18.8 %all_to_all.37 = f32[8,2,69,128]{3,1,2,0:T(2,128)S(1)} all-to-all(f32[8,2,69,128]{3,1,2,0:T(2,128)S(1)} %concatenate.55), channel_id=1, replica_groups=mesh['lvl'=8,'lon'=4] {'lvl'}, dimensions={0} | all-to-all | bytes 1130496 | tf_op jit(solution)/shard_map/all_to_all | solution.py:73
  132.9 0.9 copy.36
  (77 shorter events, 9.9 us)
Async XLA Ops:
  0.0 4.6 %copy-start.9 = (s32[256]{0:T(256)S(1)}, s32[256]{0:T(256)}, u32[]{:S(2)}) copy-start(s32[256]{0:T(256)} %param.14) | copy-start | bytes 3076
  0.0 5.3 %copy-start.6 = (bf16[3,3,192,69]{2,3,1,0:T(8,128)(2,1)S(1)}, bf16[3,3,192,69]{2,3,1,0:T(8,128)(2,1)}, u32[]{:S(2)}) copy-start(bf16[3,3,192,69]{2,3,1,0:T(8,128)(2,1)} %param.11) | copy-start | bytes 715396
  1.3 5.1 %copy-start.8 = (f32[192]{0:T(256)S(1)}, f32[192]{0:T(256)}, u32[]{:S(2)}) copy-start(f32[192]{0:T(256)} %param.13) | copy-start | bytes 2308
  1.5 7.4 %collective-permute-start = (bf16[1,16,69,1]{3,2,1,0:T(8,128)(2,1)S(1)}, bf16[1,16,69,1]{3,2,1,0:T(8,128)(2,1)S(1)}, u32[]{:S(2)}, u32[]{:S(2)}) collective-permute-start(bf16[1,16,69,1]{3,2,1,0:T(8,128)(2,1)S(1)} %get-tuple-element.13), channel_id=1, source_target_pairs={{0,1},{1,2},{2,3},{3,0},{4,5},{5,6},{6,7},{7,4},{8,9},{9,10},{10,1... | collective-permute-start | bytes 6632 | tf_op jit(solution)/shard_map/ppermute | solution.py:21
  2.0 9.3 %collective-permute-start.1 = (bf16[1,16,69,1]{3,2,1,0:T(8,128)(2,1)S(1)}, bf16[1,16,69,1]{3,2,1,0:T(8,128)(2,1)S(1)}, u32[]{:S(2)}, u32[]{:S(2)}) collective-permute-start(bf16[1,16,69,1]{3,2,1,0:T(8,128)(2,1)S(1)} %get-tuple-element.14), channel_id=1, source_target_pairs={{1,0},{2,1},{3,2},{0,3},{5,4},{6,5},{7,6},{4,7},{9,8},{10,9},{11,1... | collective-permute-start | bytes 6632 | tf_op jit(solution)/shard_map/ppermute | solution.py:24
  16.8 4.6 %collective-permute-start.2 = (bf16[1,16,192,1]{2,1,3,0:T(8,128)(2,1)S(1)}, bf16[1,16,192,1]{2,1,3,0:T(8,128)(2,1)S(1)}, u32[]{:S(2)}, u32[]{:S(2)}) collective-permute-start(bf16[1,16,192,1]{2,1,3,0:T(8,128)(2,1)S(1)} %copy.18), channel_id=1, source_target_pairs={{0,1},{1,2},{2,3},{3,0},{4,5},{5,6},{6,7},{7,4},{8,9},{9,10},{10,1... | collective-permute-start | bytes 18440 | tf_op jit(solution)/shard_map/ppermute | solution.py:21
  17.2 4.6 %collective-permute-start.3 = (bf16[1,16,192,1]{2,1,3,0:T(8,128)(2,1)S(1)}, bf16[1,16,192,1]{2,1,3,0:T(8,128)(2,1)S(1)}, u32[]{:S(2)}, u32[]{:S(2)}) collective-permute-start(bf16[1,16,192,1]{2,1,3,0:T(8,128)(2,1)S(1)} %copy.19), channel_id=1, source_target_pairs={{1,0},{2,1},{3,2},{0,3},{5,4},{6,5},{7,6},{4,7},{9,8},{10,9},{11,1... | collective-permute-start | bytes 18440 | tf_op jit(solution)/shard_map/ppermute | solution.py:24
  22.3 1.0 copy-start.4
  26.0 1.1 copy-start
  26.0 1.2 copy-start.1
  50.7 19.0 %copy-start.2 = (f32[16,69,128]{2,0,1:T(8,128)S(1)}, f32[16,69,128]{2,0,1:T(8,128)}, u32[]{:S(2)}) copy-start(f32[16,69,128]{2,0,1:T(8,128)} %param.9) | copy-start | bytes 1695748
  69.7 2.2 %copy-start.7 = (bf16[3,3,192,69]{2,3,1,0:T(8,128)(2,1)S(1)}, bf16[3,3,192,69]{2,3,1,0:T(8,128)(2,1)}, u32[]{:S(2)}) copy-start(bf16[3,3,192,69]{2,3,1,0:T(8,128)(2,1)} %param.11) | copy-start | bytes 715396
  70.1 8.9 %collective-permute-start.4 = (bf16[1,16,69,1]{3,2,1,0:T(8,128)(2,1)S(1)}, bf16[1,16,69,1]{3,2,1,0:T(8,128)(2,1)S(1)}, u32[]{:S(2)}, u32[]{:S(2)}) collective-permute-start(bf16[1,16,69,1]{3,2,1,0:T(8,128)(2,1)S(1)} %get-tuple-element.11), channel_id=1, source_target_pairs={{0,1},{1,2},{2,3},{3,0},{4,5},{5,6},{6,7},{7,4},{8,9},{9,10},{10,1... | collective-permute-start | bytes 6632 | tf_op jit(solution)/shard_map/ppermute | solution.py:21
  70.1 8.8 %collective-permute-start.5 = (bf16[1,16,69,1]{3,2,1,0:T(8,128)(2,1)S(1)}, bf16[1,16,69,1]{3,2,1,0:T(8,128)(2,1)S(1)}, u32[]{:S(2)}, u32[]{:S(2)}) collective-permute-start(bf16[1,16,69,1]{3,2,1,0:T(8,128)(2,1)S(1)} %get-tuple-element.12), channel_id=1, source_target_pairs={{1,0},{2,1},{3,2},{0,3},{5,4},{6,5},{7,6},{4,7},{9,8},{10,9},{11,1... | collective-permute-start | bytes 6632 | tf_op jit(solution)/shard_map/ppermute | solution.py:24
  84.4 3.1 %collective-permute-start.6 = (bf16[1,16,192,1]{2,1,3,0:T(8,128)(2,1)S(1)}, bf16[1,16,192,1]{2,1,3,0:T(8,128)(2,1)S(1)}, u32[]{:S(2)}, u32[]{:S(2)}) collective-permute-start(bf16[1,16,192,1]{2,1,3,0:T(8,128)(2,1)S(1)} %copy.28), channel_id=1, source_target_pairs={{0,1},{1,2},{2,3},{3,0},{4,5},{5,6},{6,7},{7,4},{8,9},{9,10},{10,1... | collective-permute-start | bytes 18440 | tf_op jit(solution)/shard_map/ppermute | solution.py:21
  85.1 3.1 %collective-permute-start.7 = (bf16[1,16,192,1]{2,1,3,0:T(8,128)(2,1)S(1)}, bf16[1,16,192,1]{2,1,3,0:T(8,128)(2,1)S(1)}, u32[]{:S(2)}, u32[]{:S(2)}) collective-permute-start(bf16[1,16,192,1]{2,1,3,0:T(8,128)(2,1)S(1)} %copy.29), channel_id=1, source_target_pairs={{1,0},{2,1},{3,2},{0,3},{5,4},{6,5},{7,6},{4,7},{9,8},{10,9},{11,1... | collective-permute-start | bytes 18440 | tf_op jit(solution)/shard_map/ppermute | solution.py:24
  88.6 1.0 copy-start.5
  113.5 19.0 %copy-start.3 = (f32[16,69,128]{2,0,1:T(8,128)S(1)}, f32[16,69,128]{2,0,1:T(8,128)}, u32[]{:S(2)}) copy-start(f32[16,69,128]{2,0,1:T(8,128)} %param.9) | copy-start | bytes 1695748
